TPU v7x, 32 devices: a whole 2x2x4 slice. The times are simulated.
32 devices in a mesh: replica: 8 (over z, y), expert: 4 (over x, core).
Axes of the slice: x: 2, y: 2, z: 4, core: 2. Of those that a mesh axis runs over, the one named last changes fastest.
Arguments:
- outer_params: float32 [28672, 4096], P('expert', 'replica'), may hold values from -6 to 6
- momentum: bfloat16 [28672, 4096], P('expert', 'replica'), may hold values from -6 to 6
- replica_deltas: bfloat16 [8, 8, 128, 4096], P('replica', 'expert'), may hold values from -6 to 6
- replica_rows: bfloat16 [8, 8, 128, 4096], P('replica', 'expert'), may hold values from -6 to 6
- block_ids: int32 [8, 8], P('replica', 'expert'), may hold values from 0 to 223, as said below
- slot_counts: int32 [8, 4], P('replica', 'expert'), may hold values from 0 to 2, as said below
Outputs:
- new_params: float32 [28672, 4096], P('expert', 'replica')
- new_momentum: bfloat16 [28672, 4096], P('expert', 'replica')
- blended_rows: bfloat16 [8, 8, 128, 4096], P('replica', 'expert')
Inputs may be any that keep to these rules, and one draw needn't show every extreme that they name: `block_ids`: within row r, slots e * 2 to (e + 1) * 2 - 1 name distinct blocks among e * 56 to (e + 1) * 56 - 1. The first slot_counts[r, e] slots of group e of row r are live, the rest are padding; in every draw some index e has 2 in every row.
All inputs are finite; a program needn't handle non-finite values.
Results may differ from a plain program's by a relative error of at most 0.0075.
Values may be sent and summed in bfloat16 or wider, within the bound.
No kernel may reach another device: no remote copies, remote signals or barrier semaphores. Data moves between devices by JAX's collectives and lax.ppermute only.
A program may use at most 128 MiB of HBM per device.

v0:
```python
import jax
import jax.numpy as jnp
from jax import lax
from jax.sharding import PartitionSpec as P

outer_rate = 0.7
nesterov_decay = 0.9
blend_weight = 0.5


def local(outer_params, momentum, replica_deltas, replica_rows, block_ids, slot_counts):
    slot_total = block_ids.shape[1]
    block_size = replica_deltas.shape[2]
    width_slab = outer_params.shape[1]
    block_count = outer_params.shape[0] // block_size
    expert_index = lax.axis_index("expert")
    all_ids, all_counts = (
        lax.all_gather(block_ids, "replica", axis=0, tiled=True),
        lax.all_gather(slot_counts, "replica", axis=0, tiled=True),
    )
    positions = jnp.arange(slot_total, dtype=jnp.int32)
    live_flags = (positions[None, :] < all_counts).reshape(-1)
    local_ids = (all_ids - expert_index * block_count).reshape(-1)
    selector = (
        local_ids[None, :] == jnp.arange(block_count, dtype=jnp.int32)[:, None]
    ) & live_flags[None, :]
    selector_float = selector.astype(jnp.float32)
    tallies = jnp.sum(selector_float, axis=1)
    received = lax.all_to_all(replica_deltas[0], "replica", split_axis=2, concat_axis=0, tiled=True)
    totals = jnp.einsum(
        "bs,sic->bic", selector.astype(jnp.bfloat16), received, preferred_element_type=jnp.float32
    )
    mean_delta = (totals / jnp.maximum(tallies, 1.0)[:, None, None]).reshape(outer_params.shape)
    moment = nesterov_decay * momentum.astype(jnp.float32) + mean_delta
    params_new = outer_params - outer_rate * (mean_delta + nesterov_decay * moment)
    blocks_new = params_new.reshape(block_count, block_size, width_slab)
    fetched = jnp.einsum(
        "bs,bic->sic", selector_float, blocks_new, precision=lax.Precision.HIGHEST
    ).astype(jnp.bfloat16)
    returned = lax.all_to_all(fetched, "replica", split_axis=0, concat_axis=2, tiled=True)
    own_flags = (positions < slot_counts[0, 0])[:, None, None]
    rows_float = replica_rows[0].astype(jnp.float32)
    mixed = blend_weight * rows_float + (1.0 - blend_weight) * returned.astype(jnp.float32)
    blended = jnp.where(own_flags, mixed, rows_float).astype(jnp.bfloat16)
    return (params_new, moment.astype(jnp.bfloat16), blended[None])


def solution(mesh):
    in_specs = (
        P("expert", "replica"),
        P("expert", "replica"),
        P("replica", "expert", None, None),
        P("replica", "expert", None, None),
        P("replica", "expert"),
        P("replica", "expert"),
    )
    out_specs = (P("expert", "replica"), P("expert", "replica"), P("replica", "expert", None, None))
    return jax.shard_map(local, mesh=mesh, in_specs=in_specs, out_specs=out_specs, check_vma=False)
```

profile of v0, /device:TPU:0, one launch (start us, length us, event | category | flops | bytes accessed | tf_op | source)
XLA Modules:
  0.0 208.3 jit_solution(10690623506712617459)
XLA Ops:
  0.6 0.0 copy-start.3
  0.6 0.0 copy-start.2
  0.7 6.2 %copy.16 = bf16[1,2,128,4096]{2,1,3,0:T(2,128)(2,1)} copy(bf16[1,2,128,4096]{3,2,1,0:T(8,128)(2,1)} %param.8) | data formatting | bytes 4194304 | tf_op args[2]
  6.8 7.3 %all-to-all-start = ((bf16[2,128,4096]{1,0,2:T(2,128)(2,1)}), bf16[2,128,4096]{1,0,2:T(2,128)(2,1)S(1)}, u32[]{:S(2)}, u32[]{:S(2)}) async-start(bf16[2,128,4096]{1,0,2:T(2,128)(2,1)} %bitcast.37), calls=%async_computation | async-start | bytes 4194304 | tf_op jit(solution)/shard_map/all_to_all | solution.py:29
  14.8 0.0 copy-done.3
  14.8 0.6 dynamic-slice
  15.4 0.7 bitcast_dynamic-update-slice_fusion
  16.1 46.5 %all-reduce = s32[8]{0:T(128)S(1)} all-reduce(s32[8]{0:T(128)S(1)} %bitcast_dynamic-update-slice_fusion), channel_id=1, replica_groups=mesh['replica'=8,'expert'=4] {'replica'}, use_global_device_ids=true, to_apply=%add | all-reduce | flops 8 | bytes 64
  62.6 0.0 copy-done.2
  62.6 18.6 %all-gather = s32[8,1,2]{2,1,0:T(1,128)S(1)} all-gather(s32[1,1,2]{2,1,0:T(1,128)S(1)} %bitcast.39), channel_id=1, replica_groups=mesh['replica'=8,'expert'=4] {'replica'}, dimensions={0}, use_global_device_ids=true | all-gather | bytes 72 | tf_op jit(solution)/shard_map/all_gather | solution.py:18
  81.2 0.1 iota_compare_fusion.1
  81.2 0.1 lt.36
  81.4 0.1 eq.15
  81.4 0.1 convert_reduce_fusion
  81.5 0.0 all-to-all-done
  81.6 5.4 %copy.17 = bf16[2,128,8,512]{3,0,2,1:T(2,128)(2,1)} copy(bf16[2,128,8,512]{1,0,3,2:T(2,128)(2,1)S(1)} %bitcast.36) | data formatting | bytes 4194304 | tf_op jit(solution)/shard_map/all_to_all | solution.py:29
  87.0 2.7 %all_to_all.23 = bf16[16,128,512]{2,0,1:T(8,128)(2,1)S(1)} reshape(bf16[8,2,128,512]{3,1,0,2:T(2,128)(2,1)} %bitcast.38) | data formatting | bytes 4194304 | tf_op jit(solution)/shard_map/all_to_all | solution.py:29
  89.7 7.6 %convolution_divide_fusion = f32[56,128,512]{2,0,1:T(8,128)} fusion(bf16[16,128,512]{2,0,1:T(8,128)(2,1)S(1)} %all_to_all.23, f32[56]{0:T(128)S(1)} %broadcast_maximum_fusion, s32[16]{0:T(128)S(1)} %eq.15, pred[16]{0:T(512)(128)(4,1)S(1)} %lt.36), kind=kOutput, calls=%fused_computation.7 | convolution fusion | flops 121112320 | bytes 16777520 | tf_op jit(solution)/shard_map/bs,sic->bic/dot_general | solution.py:30
  97.4 18.9 %copy.18 = f32[56,128,512]{2,1,0:T(8,128)} copy(f32[56,128,512]{2,0,1:T(8,128)} %convolution_divide_fusion) | data formatting | bytes 29360128 | tf_op jit(solution)/shard_map/div | solution.py:33
  116.2 15.9 %fusion.4 = (bf16[7168,512]{1,0:T(8,128)(2,1)}, f32[7168,512]{1,0:T(8,128)S(1)}) fusion(f32[56,128,512]{2,1,0:T(8,128)} %copy.18, bf16[7168,512]{1,0:T(8,128)(2,1)} %param.7, f32[7168,512]{1,0:T(8,128)} %param.6), kind=kLoop, calls=%fused_computation.6 | loop fusion | flops 29360128 | bytes 58720256 | tf_op jit(solution)/shard_map/convert_element_type | solution.py:45
  132.2 0.0 copy-start
  132.2 10.5 %fusion.7 = bf16[16,128,512]{2,0,1:T(8,128)(2,1)S(1)} fusion(f32[56,128,512]{2,1,0:T(8,128)S(1)} %bitcast.34, s32[16]{0:T(128)S(1)} %eq.15, pred[16]{0:T(512)(128)(4,1)S(1)} %lt.36), kind=kOutput, calls=%fused_computation.13 | convolution fusion | flops 705693440 | bytes 16777296 | tf_op jit(solution)/shard_map/bs,bic->sic/dot_general | solution.py:37
  142.7 0.0 copy-done
  142.7 2.5 %copy.20 = bf16[16,128,512]{2,1,0:T(8,128)(2,1)} copy(bf16[16,128,512]{2,0,1:T(8,128)(2,1)S(1)} %fusion.7) | data formatting | bytes 4194304 | tf_op jit(solution)/shard_map/convert_element_type | solution.py:39
  145.2 3.6 %all-to-all-start.1 = ((bf16[16,128,512]{2,1,0:T(8,128)(2,1)}), bf16[16,128,512]{2,1,0:T(8,128)(2,1)S(1)}, u32[]{:S(2)}, u32[]{:S(2)}) async-start(bf16[16,128,512]{2,1,0:T(8,128)(2,1)} %copy.20), calls=%async_computation.1 | async-start | bytes 4194304 | tf_op jit(solution)/shard_map/all_to_all | solution.py:40
  148.8 45.0 %all-to-all-done.1 = bf16[16,128,512]{2,1,0:T(8,128)(2,1)S(1)} async-done(((bf16[16,128,512]{2,1,0:T(8,128)(2,1)}), bf16[16,128,512]{2,1,0:T(8,128)(2,1)S(1)}, u32[]{:S(2)}, u32[]{:S(2)}) %all-to-all-start.1) | async-done | bytes 2097184 | tf_op jit(solution)/shard_map/all_to_all | solution.py:40
  193.8 0.6 convert_bitcast_fusion
  194.4 4.4 %copy.21 = f32[2,128,8,512]{3,2,1,0:T(8,128)} copy(f32[2,128,8,512]{3,1,0,2:T(8,128)S(1)} %convert_bitcast_fusion) | data formatting | bytes 8388608 | tf_op jit(solution)/shard_map/convert_element_type | solution.py:43
  198.8 0.0 copy-start.1
  198.8 5.1 %reshape.50 = f32[1,2,128,4096]{3,2,1,0:T(8,128)} reshape(f32[2,128,8,512]{3,2,1,0:T(8,128)} %copy.21) | data formatting | bytes 8388608 | tf_op jit(solution)/shard_map/convert_element_type | solution.py:43
  203.9 0.0 copy-done.1
  203.9 4.4 %fusion.6 = bf16[1,2,128,4096]{3,2,1,0:T(8,128)(2,1)} fusion(f32[1,2,128,4096]{3,2,1,0:T(8,128)} %reshape.50, bf16[1,2,128,4096]{3,2,1,0:T(8,128)(2,1)S(1)} %copy-done.1, pred[2]{0:T(512)(128)(4,1)S(1)} %iota_compare_fusion.2), kind=kLoop, calls=%fused_computation.11 | loop fusion | flops 5242880 | bytes 8388610 | tf_op jit(solution)/shard_map/convert_element_type | solution.py:44
  (4 shorter events, 0.0 us)
Async XLA Ops:
  0.6 14.2 %copy-start.3 = (u32[32]{0:T(128)S(1)}, u32[32]{0:T(128)}, u32[]{:S(2)}) copy-start(u32[32]{0:T(128)} %constant.22) | copy-start | bytes 388
  0.6 61.9 %copy-start.2 = (s32[1,2]{1,0:T(1,128)S(1)}, s32[1,2]{1,0:T(1,128)}, u32[]{:S(2)}) copy-start(s32[1,2]{1,0:T(1,128)} %param.10) | copy-start | bytes 28
  6.8 74.7 %all-to-all-start = ((bf16[2,128,4096]{1,0,2:T(2,128)(2,1)}), bf16[2,128,4096]{1,0,2:T(2,128)(2,1)S(1)}, u32[]{:S(2)}, u32[]{:S(2)}) async-start(bf16[2,128,4096]{1,0,2:T(2,128)(2,1)} %bitcast.37), calls=%async_computation | async-start | bytes 4194304 | tf_op jit(solution)/shard_map/all_to_all | solution.py:29
  132.2 10.5 %copy-start = (f32[7168,512]{1,0:T(8,128)}, f32[7168,512]{1,0:T(8,128)S(1)}, u32[]{:S(2)}) copy-start(f32[7168,512]{1,0:T(8,128)S(1)} %get-tuple-element.4) | copy-start | bytes 44040196
  145.2 48.7 %all-to-all-start.1 = ((bf16[16,128,512]{2,1,0:T(8,128)(2,1)}), bf16[16,128,512]{2,1,0:T(8,128)(2,1)S(1)}, u32[]{:S(2)}, u32[]{:S(2)}) async-start(bf16[16,128,512]{2,1,0:T(8,128)(2,1)} %copy.20), calls=%async_computation.1 | async-start | bytes 4194304 | tf_op jit(solution)/shard_map/all_to_all | solution.py:40
  198.8 5.1 %copy-start.1 = (bf16[1,2,128,4096]{3,2,1,0:T(8,128)(2,1)S(1)}, bf16[1,2,128,4096]{3,2,1,0:T(8,128)(2,1)}, u32[]{:S(2)}) copy-start(bf16[1,2,128,4096]{3,2,1,0:T(8,128)(2,1)} %param.9) | copy-start | bytes 6291460
where the time goes:
time: 209 us; the launch traced here: 208 us
  blocking collectives  65.1 us (31%)
  local copies, waits for them, and re-layouts  46.6 us (22%)
  waiting for transfers between devices  45 us (22%)
  other arithmetic  21.1 us (10%)
  matrix products  18.1 us (9%)
  starting transfers between devices  10.9 us (5%)
    unnamed x1, blocking collectives  46.5 us
    all_to_all x1, waiting for transfers between devices, local(): lax.all_to_all(fetched, 'replica', split_axis=0, concat_axis=2, tiled=True)  45 us
    div x1, local copies, waits for them, and re-layouts, local(): totals / jnp.maximum(tallies, 1.0)[:, None, None]  18.9 us
    all_gather x1, blocking collectives, local(): lax.all_gather(block_ids, 'replica', axis=0, tiled=True)  18.6 us
    convert_element_type x1, other arithmetic, local(): return (params_new, moment.astype(jnp.bfloat16), blended[None])  15.9 us
    dot_general x1, matrix products, local(): jnp.einsum('bs,bic->sic', selector_float, blocks_new, precision=lax.Preci...  10.5 us
    convert_element_type x2, local copies, waits for them, and re-layouts, local(): returned.astype(jnp.float32)  9.48 us
    all_to_all x2, local copies, waits for them, and re-layouts, local(): lax.all_to_all(replica_deltas[0], 'replica', split_axis=2, concat_axis=0,...  8.17 us
  transfers between devices with their start and end apart: 2, of which 1 were waited for; matrix products, arithmetic and copies ran while one was open for 1% of the time, Pallas kernels for 0%

commit v1 on v0

v1 whole, which is shorter than its diff:
```python
import functools

import jax
import jax.numpy as jnp
from jax import lax
from jax.experimental import pallas as pl
from jax.experimental.pallas import tpu as pltpu
from jax.sharding import PartitionSpec as P

outer_rate = 0.7
nesterov_decay = 0.9
blend_weight = 0.5


HBM = pl.BlockSpec(memory_space=pltpu.HBM)
ANY = pl.BlockSpec(memory_space=pl.ANY)
SMEM = pl.BlockSpec(memory_space=pltpu.SMEM)
VMEM = pl.BlockSpec(memory_space=pltpu.VMEM)
DMA = pltpu.SemaphoreType.DMA
BLOCK_BYTES = 1 << 20
PARTS = 2


def peer_of(me, k, n):
    return me ^ k if n & (n - 1) == 0 else (k - me) % n


def rounds_of(n):
    return sorted(range(n), key=lambda k: (k < n // 2, -(k < n // 2) * (n - k), k))


def peer_in_kernel(k, n):
    me = lax.axis_index("replica")
    return me ^ k if n & (n - 1) == 0 else lax.rem(k - me + n, n)


def step_of(mean, momentum, params):
    moment = nesterov_decay * momentum.astype(jnp.float32) + mean
    return moment, params - outer_rate * (mean + nesterov_decay * moment)


def columns_of(k, n, width):
    return pl.ds(pl.multiple_of(peer_in_kernel(k, n) * width, width), width)


def pack_kernel(start, deltas, *rest):
    packed, sems = rest[:-1], rest[-1]
    n, (_, rows, width) = len(packed), packed[0].shape
    copies = [
        pltpu.make_async_copy(
            deltas.at[:, pl.ds(start, rows), columns_of(k, n, width)], packed[k], sems.at[k]
        )
        for k in range(n)
    ]
    for copy in copies:
        copy.start()
    for copy in copies:
        copy.wait()


def pack(deltas, start, rows, n):
    slots, _, total = deltas.shape
    return pl.pallas_call(
        functools.partial(pack_kernel, start),
        name="pack",
        in_specs=[HBM],
        out_specs=[VMEM] * n,
        out_shape=[jax.ShapeDtypeStruct((slots, rows, total // n), deltas.dtype)] * n,
        scratch_shapes=[DMA((n,))],
    )(deltas)


def listed_body(start, block_size, block_count, n, *refs):
    facts, params, momentum = refs[:3]
    received, fetched, means = refs[3 : 3 + n], refs[3 + n : 3 + 2 * n], refs[3 + 2 * n]
    ids, keys, got, held, moved, total, sent, got_sems, held_sems, moved_sems, mean_sems, sent_sems = refs[4 + 2 * n :]
    entries, rows, width = held.shape
    slots = entries // n
    base = lax.axis_index("expert") * block_count

    def place(s):
        return pl.ds(pl.multiple_of(ids[s] * block_size + start, 16), rows)

    def pair(s):
        return (
            pltpu.make_async_copy(params.at[place(s), :], held.at[s], held_sems.at[s]),
            pltpu.make_async_copy(momentum.at[place(s), :], moved.at[s], moved_sems.at[s]),
        )

    arrivals = [
        pltpu.make_async_copy(received[k], got.at[pl.ds(k * slots, slots)], got_sems.at[k]) for k in range(n)
    ]
    for k in range(n):
        arrivals[k].start()
        replica = peer_in_kernel(k, n)
        for j in range(slots):
            s = k * slots + j
            mine = facts[replica, j] - base
            ids[s] = mine
            keys[s] = jnp.where(facts[replica, slots] > j, mine, -1)
            for copy in pair(s):
                copy.start()
    for copy in arrivals:
        copy.wait()

    def work(s, carry):
        mine = ids[s]
        live = (keys[s] == mine).astype(jnp.int32)
        total[s] = got[s].astype(jnp.float32) * live.astype(jnp.float32)

        def add(other, tally):
            match = jnp.logical_and(keys[other] == mine, other != s)

            @pl.when(match)
            def _():
                total[s] += got[other].astype(jnp.float32)

            return tally + match.astype(jnp.int32)

        tally = lax.fori_loop(0, entries, add, live, unroll=8)
        scale = 1.0 / jnp.full((1, width), jnp.maximum(tally, 1).astype(jnp.float32))
        mean = total[s] * scale
        for copy in pair(s):
            copy.wait()
        _, updated = step_of(mean, moved[s], held[s])
        sent[s] = updated.astype(sent.dtype)
        total[s] = mean
        pltpu.make_async_copy(total.at[s], means.at[s], mean_sems.at[s]).start()
        return carry

    lax.fori_loop(0, entries, work, 0)
    leaves = [
        pltpu.make_async_copy(sent.at[pl.ds(k * slots, slots)], fetched[k], sent_sems.at[k]) for k in range(n)
    ]
    for copy in leaves:
        copy.start()

    def end(s, carry):
        pltpu.make_async_copy(total.at[s], means.at[s], mean_sems.at[s]).wait()
        return carry

    lax.fori_loop(0, entries, end, 0)
    for copy in leaves:
        copy.wait()


def listed(start, block_size, facts, params, momentum, received):
    n, (slots, rows, width) = len(received), received[0].shape
    entries = n * slots
    shape = (entries, rows, width)
    out = pl.pallas_call(
        functools.partial(listed_body, start, block_size, params.shape[0] // block_size, n),
        name="listed",
        in_specs=[SMEM, HBM, HBM] + [ANY] * n,
        out_specs=[ANY] * (n + 1),
        out_shape=[jax.ShapeDtypeStruct(piece.shape, piece.dtype) for piece in received]
        + [jax.ShapeDtypeStruct(shape, jnp.float32)],
        scratch_shapes=[
            pltpu.SMEM((entries,), jnp.int32),
            pltpu.SMEM((entries,), jnp.int32),
            pltpu.VMEM(shape, received[0].dtype),
            pltpu.VMEM(shape, params.dtype),
            pltpu.VMEM(shape, momentum.dtype),
            pltpu.VMEM(shape, jnp.float32),
            pltpu.VMEM(shape, received[0].dtype),
            DMA((n,)), DMA((entries,)), DMA((entries,)), DMA((entries,)), DMA((n,)),
        ],
        cost_estimate=pl.CostEstimate(
            flops=10 * entries * rows * width, bytes_accessed=16 * entries * rows * width, transcendentals=0
        ),
    )(facts, params, momentum, *received)
    return out[:n], out[n]


def update_body(block_size, block_count, group, n, parts, facts, params, momentum, *refs):
    means, (params_new, momentum_new) = refs[:parts], refs[parts:]
    entries, rows, _ = means[0].shape
    slots = entries // n
    first = lax.axis_index("expert") * block_count + pl.program_id(0) * group
    moment, updated = step_of(0.0, momentum[...], params[...])
    params_new[...] = updated
    momentum_new[...] = moment.astype(momentum_new.dtype)
    for k in range(n):
        replica = peer_in_kernel(k, n)
        for j in range(slots):
            where = facts[replica, j] - first

            @pl.when(jnp.logical_and(where >= 0, where < group))
            def _(where=where, s=k * slots + j):
                for part in range(parts):
                    span = pl.ds(pl.multiple_of(where * block_size + part * rows, 16), rows)
                    moment, updated = step_of(means[part][s], momentum[span, :], params[span, :])
                    params_new[span, :] = updated
                    momentum_new[span, :] = moment.astype(momentum_new.dtype)


def update(block_size, facts, params, momentum, means):
    rows, width = params.shape
    count = rows // block_size
    group = max(
        k for k in range(1, count + 1)
        if count % k == 0 and (k == 1 or k * block_size * width * 4 <= BLOCK_BYTES)
    )
    spec = pl.BlockSpec((group * block_size, width), lambda i: (i, 0))
    return pl.pallas_call(
        functools.partial(update_body, block_size, count, group, facts.shape[0], len(means)),
        name="update",
        grid=(count // group,),
        in_specs=[SMEM, spec, spec] + [VMEM] * len(means),
        out_specs=[spec, spec],
        out_shape=[
            jax.ShapeDtypeStruct(params.shape, params.dtype),
            jax.ShapeDtypeStruct(momentum.shape, momentum.dtype),
        ],
        cost_estimate=pl.CostEstimate(
            flops=6 * rows * width, bytes_accessed=12 * rows * width, transcendentals=0
        ),
    )(facts, params, momentum, *means)


def blend_body(start, n, count, rows_in, *rest):
    returned, blended = rest[:n], rest[-6]
    got, own, mixed, load_sems, got_sems = rest[-5:-2] + (rest[-2], rest[-1])
    _, slots, rows, width = got.shape
    span = pl.ds(start, rows)
    loads = [
        pltpu.make_async_copy(rows_in.at[:, span, columns_of(k, n, width)], own.at[k], load_sems.at[k])
        for k in range(n)
    ]
    arrivals = [pltpu.make_async_copy(returned[k], got.at[k], got_sems.at[k]) for k in range(n)]
    stores = [
        pltpu.make_async_copy(mixed.at[k], blended.at[:, span, columns_of(k, n, width)], load_sems.at[k])
        for k in range(n)
    ]
    for k in range(n):
        loads[k].start()
        arrivals[k].start()
    for k in range(n):
        loads[k].wait()
        arrivals[k].wait()
        for j in range(slots):
            rows_float = own[k, j].astype(jnp.float32)
            both = blend_weight * rows_float + (1.0 - blend_weight) * got[k, j].astype(jnp.float32)
            mixed[k, j] = jnp.where(count[0] > j, both, rows_float).astype(mixed.dtype)
        stores[k].start()
    for copy in stores:
        copy.wait()


def blend(start, count, returned, rows_in, blended):
    n, (slots, rows, width) = len(returned), returned[0].shape
    before = [] if blended is None else [blended]
    scratch = pltpu.VMEM((n, slots, rows, width), rows_in.dtype)
    return pl.pallas_call(
        functools.partial(blend_body, start, n),
        name="blend",
        in_specs=[SMEM, HBM] + [ANY] * n + [HBM] * len(before),
        out_specs=HBM,
        out_shape=jax.ShapeDtypeStruct(rows_in.shape, rows_in.dtype),
        input_output_aliases={2 + n: 0} if before else {},
        scratch_shapes=[scratch, scratch, scratch, DMA((n,)), DMA((n,))],
    )(count, rows_in, *returned, *before)


def local(outer_params, momentum, replica_deltas, replica_rows, block_ids, slot_counts):
    n = lax.axis_size("replica")
    slots = block_ids.shape[1]
    block_size = replica_deltas.shape[2]
    rows = block_size // PARTS
    deltas, own_rows = replica_deltas[0], replica_rows[0]

    def exchange(pieces):
        out = list(pieces)
        for k in rounds_of(n):
            if k:
                out[k] = lax.ppermute(pieces[k], "replica", [(i, peer_of(i, k, n)) for i in range(n)])
        return out

    received = []
    for part in range(PARTS):
        packed = pack(deltas, part * rows, rows, n)
        received.append(exchange(packed))
    facts = jnp.concatenate([block_ids, slot_counts], axis=1)
    facts = lax.all_to_all(jnp.broadcast_to(facts, (n, slots + 1)), "replica", 0, 0, tiled=True)
    returned, means = [], []
    for part in range(PARTS):
        fetched, mean = listed(part * rows, block_size, facts, outer_params, momentum, received[part])
        means.append(mean)
        returned.append(exchange(fetched))
    params_new, momentum_new = update(block_size, facts, outer_params, momentum, means)
    blended = None
    for part in range(PARTS):
        blended = blend(part * rows, slot_counts[0], returned[part], own_rows, blended)
    return params_new, momentum_new, blended[None]


def solution(mesh):
    in_specs = (
        P("expert", "replica"),
        P("expert", "replica"),
        P("replica", "expert", None, None),
        P("replica", "expert", None, None),
        P("replica", "expert"),
        P("replica", "expert"),
    )
    out_specs = (P("expert", "replica"), P("expert", "replica"), P("replica", "expert", None, None))
    return jax.shard_map(local, mesh=mesh, in_specs=in_specs, out_specs=out_specs, check_vma=False)
```

time: 209 us -> 135 us (0.65)
  blocking collectives: 65.1 us -> 0 us
  starting transfers between devices: 10.9 us -> 60.9 us
  Pallas kernels: 0 us -> 49.7 us
  local copies, waits for them, and re-layouts: 46.6 us -> 2.03 us
  waiting for transfers between devices: 45 us -> 19.8 us
  other arithmetic: 21.1 us -> 0.08 us
  matrix products: 18.1 us -> 0 us
    ppermute x0 -> x28, starting transfers between devices: none -> 55.3 us  [exchange(): lax.ppermute(pieces[k], 'replica', [(i, peer_of(i, k, n)) for i in range(...]
    pallas_call x0 -> x7, Pallas kernels: none -> 49.7 us  [the longest x1 23.4 us: update(): pl.pallas_call(functools.partial(update_body, block_size, count, group, f...]
    unnamed x1 -> x0, blocking collectives: 46.5 us -> none
    all_to_all x2 -> x1, waiting for transfers between devices: 45 us -> 5.94 us  [local(): lax.all_to_all(jnp.broadcast_to(facts, (n, slots + 1)), 'replica', 0, 0,...]
    convert_element_type x3 -> x0, other arithmetic: 20.9 us -> none  [the longest x1 15.9 us: local(): return (params_new, moment.astype(jnp.bfloat16), blended[None])]
    div x1 -> x0, local copies, waits for them, and re-layouts: 18.9 us -> none  [local(): totals / jnp.maximum(tallies, 1.0)[:, None, None]]
    all_gather x1 -> x0, blocking collectives: 18.6 us -> none  [local(): lax.all_gather(block_ids, 'replica', axis=0, tiled=True)]
    dot_general x2 -> x0, matrix products: 18.1 us -> none  [the longest x1 10.5 us: local(): jnp.einsum('bs,bic->sic', selector_float, blocks_new, precision=lax.Preci...]
  transfers between devices with their start and end apart: 2 -> 29, of which waited for: 1 -> 5; matrix products, arithmetic and copies ran while one was open for 1% -> 1% of each run, Pallas kernels for 0% -> 33%
where the time goes in v1:
time: 135 us; the launch traced here: 134 us
  starting transfers between devices  60.9 us (45%)
  Pallas kernels  49.7 us (37%)
  waiting for transfers between devices  19.8 us (15%)
  local copies, waits for them, and re-layouts  2.03 us (2%)
  between operations  1.75 us (1%)
    ppermute x28, starting transfers between devices, exchange(): lax.ppermute(pieces[k], 'replica', [(i, peer_of(i, k, n)) for i in range(...  55.3 us
    pallas_call x1, Pallas kernels, update(): pl.pallas_call(functools.partial(update_body, block_size, count, group, f...  23.4 us
    pallas_call x2, Pallas kernels, listed(): pl.pallas_call(functools.partial(listed_body, start, block_size, params.s...  16.7 us
    ppermute x28, waiting for transfers between devices, exchange(): lax.ppermute(pieces[k], 'replica', [(i, peer_of(i, k, n)) for i in range(...  13.8 us
    all_to_all x1, waiting for transfers between devices, local(): lax.all_to_all(jnp.broadcast_to(facts, (n, slots + 1)), 'replica', 0, 0,...  5.94 us
    all_to_all x1, starting transfers between devices, local(): lax.all_to_all(jnp.broadcast_to(facts, (n, slots + 1)), 'replica', 0, 0,...  5.58 us
    pallas_call x2, Pallas kernels, blend(): pl.pallas_call(functools.partial(blend_body, start, n), name='blend', in_...  4.93 us
    pallas_call x2, Pallas kernels, pack(): pl.pallas_call(functools.partial(pack_kernel, start), name='pack', in_spe...  4.68 us
  transfers between devices with their start and end apart: 29, of which 5 were waited for; matrix products, arithmetic and copies ran while one was open for 1% of the time, Pallas kernels for 33%

profile of v1, /device:TPU:0, one launch (start us, length us, event | category | flops | bytes accessed | tf_op | source)
XLA Modules:
  0.0 134.1 jit_solution(3082731896960315734)
XLA Ops:
  0.6 2.4 %pack.3 = (bf16[2,64,512]{2,1,0:T(8,128)(2,1)}, bf16[2,64,512]{2,1,0:T(8,128)(2,1)}, bf16[2,64,512]{2,1,0:T(8,128)(2,1)}, bf16[2,64,512]{2,1,0:T(8,128)(2,1)}, b...) custom-call(bf16[2,128,4096]{2,1,0:T(8,128)(2,1)} %bitcast.9), custom_call_target="tpu_custom_call" | custom-call | tf_op jit(solution)/shard_map/pack/pallas_call | solution.py:63
  3.1 3.1 %collective-permute-start.7 = (bf16[2,64,512]{2,1,0:T(8,128)(2,1)}, bf16[2,64,512]{2,1,0:T(8,128)(2,1)S(1)}, u32[]{:S(2)}, u32[]{:S(2)}) collective-permute-start(bf16[2,64,512]{2,1,0:T(8,128)(2,1)} %get-tuple-element.49), channel_id=1, source_target_pairs={{0,4},{4,0},{8,12},{12,8},{16,20},{20,16},{24,28},{28,24},{1,5},{5... | collective-permute-start | bytes 393224 | tf_op jit(solution)/shard_map/ppermute | solution.py:276
  6.1 1.6 %collective-permute-start.8 = (bf16[2,64,512]{2,1,0:T(8,128)(2,1)}, bf16[2,64,512]{2,1,0:T(8,128)(2,1)S(1)}, u32[]{:S(2)}, u32[]{:S(2)}) collective-permute-start(bf16[2,64,512]{2,1,0:T(8,128)(2,1)} %get-tuple-element.50), channel_id=1, source_target_pairs={{0,8},{4,12},{8,0},{12,4},{16,24},{20,28},{24,16},{28,20},{1,9},{5... | collective-permute-start | bytes 393224 | tf_op jit(solution)/shard_map/ppermute | solution.py:276
  7.7 2.3 %pack.2 = (bf16[2,64,512]{2,1,0:T(8,128)(2,1)}, bf16[2,64,512]{2,1,0:T(8,128)(2,1)}, bf16[2,64,512]{2,1,0:T(8,128)(2,1)}, bf16[2,64,512]{2,1,0:T(8,128)(2,1)}, b...) custom-call(bf16[2,128,4096]{2,1,0:T(8,128)(2,1)} %bitcast.10), custom_call_target="tpu_custom_call" | custom-call | tf_op jit(solution)/shard_map/pack/pallas_call | solution.py:63
  10.6 3.0 %collective-permute-start.2 = (bf16[2,64,512]{2,1,0:T(8,128)(2,1)}, bf16[2,64,512]{2,1,0:T(8,128)(2,1)S(1)}, u32[]{:S(2)}, u32[]{:S(2)}) collective-permute-start(bf16[2,64,512]{2,1,0:T(8,128)(2,1)} %get-tuple-element.42), channel_id=1, source_target_pairs={{0,12},{4,8},{8,4},{12,0},{16,28},{20,24},{24,20},{28,16},{1,13},{... | collective-permute-start | bytes 393224 | tf_op jit(solution)/shard_map/ppermute | solution.py:276
  13.6 2.6 %collective-permute-start.3 = (bf16[2,64,512]{2,1,0:T(8,128)(2,1)}, bf16[2,64,512]{2,1,0:T(8,128)(2,1)S(1)}, u32[]{:S(2)}, u32[]{:S(2)}) collective-permute-start(bf16[2,64,512]{2,1,0:T(8,128)(2,1)} %get-tuple-element.43), channel_id=1, source_target_pairs={{0,16},{4,20},{8,24},{12,28},{16,0},{20,4},{24,8},{28,12},{1,17},{... | collective-permute-start | bytes 393224 | tf_op jit(solution)/shard_map/ppermute | solution.py:276
  16.5 2.5 %collective-permute-start.5 = (bf16[2,64,512]{2,1,0:T(8,128)(2,1)}, bf16[2,64,512]{2,1,0:T(8,128)(2,1)S(1)}, u32[]{:S(2)}, u32[]{:S(2)}) collective-permute-start(bf16[2,64,512]{2,1,0:T(8,128)(2,1)} %get-tuple-element.45), channel_id=1, source_target_pairs={{0,24},{4,28},{8,16},{12,20},{16,8},{20,12},{24,0},{28,4},{1,25},{... | collective-permute-start | bytes 393224 | tf_op jit(solution)/shard_map/ppermute | solution.py:276
  18.9 4.0 %collective-permute-start.6 = (bf16[2,64,512]{2,1,0:T(8,128)(2,1)}, bf16[2,64,512]{2,1,0:T(8,128)(2,1)S(1)}, u32[]{:S(2)}, u32[]{:S(2)}) collective-permute-start(bf16[2,64,512]{2,1,0:T(8,128)(2,1)} %get-tuple-element.46), channel_id=1, source_target_pairs={{0,28},{4,24},{8,20},{12,16},{16,12},{20,8},{24,4},{28,0},{1,29},{... | collective-permute-start | bytes 393224 | tf_op jit(solution)/shard_map/ppermute | solution.py:276
  23.5 7.7 %collective-permute-done.3.refs_7_ = bf16[2,64,512]{2,1,0:T(8,128)(2,1)S(1)} collective-permute-done((bf16[2,64,512]{2,1,0:T(8,128)(2,1)}, bf16[2,64,512]{2,1,0:T(8,128)(2,1)S(1)}, u32[]{:S(2)}, u32[]{:S(2)}) %collective-permute-start.3) | collective-permute-done | bytes 131104 | tf_op jit(solution)/shard_map/ppermute | solution.py:276
  31.2 4.6 %collective-permute-done.4.refs_8_ = bf16[2,64,512]{2,1,0:T(8,128)(2,1)S(1)} collective-permute-done((bf16[2,64,512]{2,1,0:T(8,128)(2,1)}, bf16[2,64,512]{2,1,0:T(8,128)(2,1)S(1)}, u32[]{:S(2)}, u32[]{:S(2)}) %collective-permute-start.4) | collective-permute-done | bytes 131104 | tf_op jit(solution)/shard_map/ppermute | solution.py:276
  35.9 6.7 %collective-permute-start.12 = (bf16[2,64,512]{2,1,0:T(8,128)(2,1)S(1)}, bf16[2,64,512]{2,1,0:T(8,128)(2,1)S(1)}, u32[]{:S(2)}, u32[]{:S(2)}) collective-permute-start(bf16[2,64,512]{2,1,0:T(8,128)(2,1)S(1)} %copy-done.30), channel_id=1, source_target_pairs={{0,24},{4,28},{8,16},{12,20},{16,8},{20,12},{24,0},{28,4},{1,25},{... | collective-permute-start | bytes 393224 | tf_op jit(solution)/shard_map/ppermute | solution.py:276
  43.9 5.6 %all-to-all-start = ((s32[8,1,3]{2,1,0:T(1,128)}), s32[8,1,3]{2,1,0:T(1,128)S(1)}, u32[]{:S(2)}, u32[]{:S(2)}) async-start(s32[8,1,3]{2,1,0:T(1,128)} %broadcast_in_dim.8), calls=%async_computation | async-start | bytes 8192 | tf_op jit(solution)/shard_map/all_to_all | solution.py:284
  49.5 4.8 %collective-permute-start.13 = (bf16[2,64,512]{2,1,0:T(8,128)(2,1)S(1)}, bf16[2,64,512]{2,1,0:T(8,128)(2,1)S(1)}, u32[]{:S(2)}, u32[]{:S(2)}) collective-permute-start(bf16[2,64,512]{2,1,0:T(8,128)(2,1)S(1)} %copy-done.29), channel_id=1, source_target_pairs={{0,28},{4,24},{8,20},{12,16},{16,12},{20,8},{24,4},{28,0},{1,29},{... | collective-permute-start | bytes 393224 | tf_op jit(solution)/shard_map/ppermute | solution.py:276
  54.3 5.9 %all-to-all-done = s32[8,1,3]{2,1,0:T(1,128)S(1)} async-done(((s32[8,1,3]{2,1,0:T(1,128)}), s32[8,1,3]{2,1,0:T(1,128)S(1)}, u32[]{:S(2)}, u32[]{:S(2)}) %all-to-all-start) | async-done | bytes 128 | tf_op jit(solution)/shard_map/all_to_all | solution.py:284
  60.8 8.2 %listed.2 = (bf16[2,64,512]{2,1,0:T(8,128)(2,1)}, bf16[2,64,512]{2,1,0:T(8,128)(2,1)}, bf16[2,64,512]{2,1,0:T(8,128)(2,1)}, bf16[2,64,512]{2,1,0:T(8,128)(2,1)},...) custom-call(s32[8,3]{1,0:T(8,128)} %bitcast.14, ...), custom_call_target="tpu_custom_call" | custom-call | flops 5242880 | bytes 8388608 | tf_op jit(solution)/shard_map/listed/pallas_call | solution.py:151
  69.1 1.5 %collective-permute-start.21 = (bf16[2,64,512]{2,1,0:T(8,128)(2,1)}, bf16[2,64,512]{2,1,0:T(8,128)(2,1)S(1)}, u32[]{:S(2)}, u32[]{:S(2)}) collective-permute-start(bf16[2,64,512]{2,1,0:T(8,128)(2,1)} %get-tuple-element.68), channel_id=1, source_target_pairs={{0,4},{4,0},{8,12},{12,8},{16,20},{20,16},{24,28},{28,24},{1,5},{5... | collective-permute-start | bytes 393224 | tf_op jit(solution)/shard_map/ppermute | solution.py:276
  71.2 1.5 %collective-permute-start.23 = (bf16[2,64,512]{2,1,0:T(8,128)(2,1)}, bf16[2,64,512]{2,1,0:T(8,128)(2,1)S(1)}, u32[]{:S(2)}, u32[]{:S(2)}) collective-permute-start(bf16[2,64,512]{2,1,0:T(8,128)(2,1)} %get-tuple-element.70), channel_id=1, source_target_pairs={{0,12},{4,8},{8,4},{12,0},{16,28},{20,24},{24,20},{28,16},{1,13},{... | collective-permute-start | bytes 393224 | tf_op jit(solution)/shard_map/ppermute | solution.py:276
  72.7 0.8 collective-permute-start.24
  73.6 3.0 %collective-permute-start.25 = (bf16[2,64,512]{2,1,0:T(8,128)(2,1)}, bf16[2,64,512]{2,1,0:T(8,128)(2,1)S(1)}, u32[]{:S(2)}, u32[]{:S(2)}) collective-permute-start(bf16[2,64,512]{2,1,0:T(8,128)(2,1)} %get-tuple-element.72), channel_id=1, source_target_pairs={{0,20},{4,16},{8,28},{12,24},{16,4},{20,0},{24,12},{28,8},{1,21},{... | collective-permute-start | bytes 393224 | tf_op jit(solution)/shard_map/ppermute | solution.py:276
  76.6 8.4 %listed.3 = (bf16[2,64,512]{2,1,0:T(8,128)(2,1)}, bf16[2,64,512]{2,1,0:T(8,128)(2,1)}, bf16[2,64,512]{2,1,0:T(8,128)(2,1)}, bf16[2,64,512]{2,1,0:T(8,128)(2,1)},...) custom-call(s32[8,3]{1,0:T(8,128)} %bitcast.15, ...), custom_call_target="tpu_custom_call" | custom-call | flops 5242880 | bytes 8388608 | tf_op jit(solution)/shard_map/listed/pallas_call | solution.py:151
  85.0 1.7 %collective-permute-start.26 = (bf16[2,64,512]{2,1,0:T(8,128)(2,1)S(1)}, bf16[2,64,512]{2,1,0:T(8,128)(2,1)S(1)}, u32[]{:S(2)}, u32[]{:S(2)}) collective-permute-start(bf16[2,64,512]{2,1,0:T(8,128)(2,1)S(1)} %copy-done.35), channel_id=1, source_target_pairs={{0,24},{4,28},{8,16},{12,20},{16,8},{20,12},{24,0},{28,4},{1,25},{... | collective-permute-start | bytes 393224 | tf_op jit(solution)/shard_map/ppermute | solution.py:276
  86.8 2.2 %collective-permute-start.27 = (bf16[2,64,512]{2,1,0:T(8,128)(2,1)S(1)}, bf16[2,64,512]{2,1,0:T(8,128)(2,1)S(1)}, u32[]{:S(2)}, u32[]{:S(2)}) collective-permute-start(bf16[2,64,512]{2,1,0:T(8,128)(2,1)S(1)} %copy-done.34), channel_id=1, source_target_pairs={{0,28},{4,24},{8,20},{12,16},{16,12},{20,8},{24,4},{28,0},{1,29},{... | collective-permute-start | bytes 393224 | tf_op jit(solution)/shard_map/ppermute | solution.py:276
  89.0 1.5 %collective-permute-start.14 = (bf16[2,64,512]{2,1,0:T(8,128)(2,1)}, bf16[2,64,512]{2,1,0:T(8,128)(2,1)S(1)}, u32[]{:S(2)}, u32[]{:S(2)}) collective-permute-start(bf16[2,64,512]{2,1,0:T(8,128)(2,1)} %get-tuple-element.60), channel_id=1, source_target_pairs={{0,4},{4,0},{8,12},{12,8},{16,20},{20,16},{24,28},{28,24},{1,5},{5... | collective-permute-start | bytes 393224 | tf_op jit(solution)/shard_map/ppermute | solution.py:276
  90.5 2.0 %collective-permute-start.16 = (bf16[2,64,512]{2,1,0:T(8,128)(2,1)}, bf16[2,64,512]{2,1,0:T(8,128)(2,1)S(1)}, u32[]{:S(2)}, u32[]{:S(2)}) collective-permute-start(bf16[2,64,512]{2,1,0:T(8,128)(2,1)} %get-tuple-element.62), channel_id=1, source_target_pairs={{0,12},{4,8},{8,4},{12,0},{16,28},{20,24},{24,20},{28,16},{1,13},{... | collective-permute-start | bytes 393224 | tf_op jit(solution)/shard_map/ppermute | solution.py:276
  92.5 2.2 %collective-permute-start.17 = (bf16[2,64,512]{2,1,0:T(8,128)(2,1)}, bf16[2,64,512]{2,1,0:T(8,128)(2,1)S(1)}, u32[]{:S(2)}, u32[]{:S(2)}) collective-permute-start(bf16[2,64,512]{2,1,0:T(8,128)(2,1)} %get-tuple-element.63), channel_id=1, source_target_pairs={{0,16},{4,20},{8,24},{12,28},{16,0},{20,4},{24,8},{28,12},{1,17},{... | collective-permute-start | bytes 393224 | tf_op jit(solution)/shard_map/ppermute | solution.py:276
  94.7 0.9 collective-permute-done.27.rest_7_
  95.6 4.8 %collective-permute-start.18 = (bf16[2,64,512]{2,1,0:T(8,128)(2,1)}, bf16[2,64,512]{2,1,0:T(8,128)(2,1)S(1)}, u32[]{:S(2)}, u32[]{:S(2)}) collective-permute-start(bf16[2,64,512]{2,1,0:T(8,128)(2,1)} %get-tuple-element.64), channel_id=1, source_target_pairs={{0,20},{4,16},{8,28},{12,24},{16,4},{20,0},{24,12},{28,8},{1,21},{... | collective-permute-start | bytes 393224 | tf_op jit(solution)/shard_map/ppermute | solution.py:276
  100.4 2.5 %collective-permute-start.19 = (bf16[2,64,512]{2,1,0:T(8,128)(2,1)}, bf16[2,64,512]{2,1,0:T(8,128)(2,1)S(1)}, u32[]{:S(2)}, u32[]{:S(2)}) collective-permute-start(bf16[2,64,512]{2,1,0:T(8,128)(2,1)} %get-tuple-element.65), channel_id=1, source_target_pairs={{0,24},{4,28},{8,16},{12,20},{16,8},{20,12},{24,0},{28,4},{1,25},{... | collective-permute-start | bytes 393224 | tf_op jit(solution)/shard_map/ppermute | solution.py:276
  102.9 2.0 %collective-permute-start.20 = (bf16[2,64,512]{2,1,0:T(8,128)(2,1)}, bf16[2,64,512]{2,1,0:T(8,128)(2,1)S(1)}, u32[]{:S(2)}, u32[]{:S(2)}) collective-permute-start(bf16[2,64,512]{2,1,0:T(8,128)(2,1)} %get-tuple-element.66), channel_id=1, source_target_pairs={{0,28},{4,24},{8,20},{12,16},{16,12},{20,8},{24,4},{28,0},{1,29},{... | collective-permute-start | bytes 393224 | tf_op jit(solution)/shard_map/ppermute | solution.py:276
  104.9 23.4 %update.1 = (f32[7168,512]{1,0:T(8,128)}, bf16[7168,512]{1,0:T(8,128)(2,1)}) custom-call(s32[8,3]{1,0:T(8,128)} %bitcast.16, f32[7168,512]{1,0:T(8,128)} %params.1, bf16[7168,512]{1,0:T(8,128)(2,1)} %momentum.1, f32[16,64,512]{2,1,0:T(8,128)} %get-tuple-element.47.refs_0_, f32[16,64,512]{2,1,0:T(8,128)} %get-tuple-element.56.refs_1_), custom_call_target="tpu_custom_call" | custom-call | flops 22020096 | bytes 44040192 | tf_op jit(solution)/shard_map/update/pallas_call | solution.py:205
  128.3 2.5 %blend.2.rest_8_ = bf16[2,128,4096]{2,1,0:T(8,128)(2,1)} custom-call(s32[1]{0:T(128)} %bitcast.7.count, bf16[2,128,4096]{2,1,0:T(8,128)(2,1)} %bitcast.11, bf16[2,64,512]{2,1,0:T(8,128)(2,1)} %get-tuple-element.67.rest_0_, bf16[2,64,512]{2,1,0:T(8,128)(2,1)} %copy-done.14, bf16[2,64,512]{2,1,0:T(8,128)(2,1)} %copy-done.15, bf16[2,64,512]{2,1,0:T(8,128)(2,1)} %copy-done.16, ...), custom_call_target="tpu_custom_call" | custom-call | tf_op jit(solution)/shard_map/blend/pallas_call | solution.py:254
  131.7 2.5 %blend.3 = bf16[2,128,4096]{2,1,0:T(8,128)(2,1)} custom-call(s32[1]{0:T(128)} %bitcast.8.count, bf16[2,128,4096]{2,1,0:T(8,128)(2,1)} %bitcast.12, bf16[2,64,512]{2,1,0:T(8,128)(2,1)} %get-tuple-element.59.rest_0_, bf16[2,64,512]{2,1,0:T(8,128)(2,1)} %copy-done.21, bf16[2,64,512]{2,1,0:T(8,128)(2,1)} %copy-done.22, ...), custom_call_target="tpu_custom_call", output_to_operand_aliasing={{}: (10, {})} | custom-call | tf_op jit(solution)/shard_map/blend/pallas_call | solution.py:254
  (109 shorter events, 4.1 us)
Async XLA Ops:
  3.1 46.4 %copy-start.29 = (bf16[2,64,512]{2,1,0:T(8,128)(2,1)S(1)}, bf16[2,64,512]{2,1,0:T(8,128)(2,1)}, u32[]{:S(2)}) copy-start(bf16[2,64,512]{2,1,0:T(8,128)(2,1)} %get-tuple-element.55) | copy-start | bytes 393220
  3.1 10.5 %collective-permute-start.7 = (bf16[2,64,512]{2,1,0:T(8,128)(2,1)}, bf16[2,64,512]{2,1,0:T(8,128)(2,1)S(1)}, u32[]{:S(2)}, u32[]{:S(2)}) collective-permute-start(bf16[2,64,512]{2,1,0:T(8,128)(2,1)} %get-tuple-element.49), channel_id=1, source_target_pairs={{0,4},{4,0},{8,12},{12,8},{16,20},{20,16},{24,28},{28,24},{1,5},{5... | collective-permute-start | bytes 393224 | tf_op jit(solution)/shard_map/ppermute | solution.py:276
  6.1 10.0 %collective-permute-start.8 = (bf16[2,64,512]{2,1,0:T(8,128)(2,1)}, bf16[2,64,512]{2,1,0:T(8,128)(2,1)S(1)}, u32[]{:S(2)}, u32[]{:S(2)}) collective-permute-start(bf16[2,64,512]{2,1,0:T(8,128)(2,1)} %get-tuple-element.50), channel_id=1, source_target_pairs={{0,8},{4,12},{8,0},{12,4},{16,24},{20,28},{24,16},{28,20},{1,9},{5... | collective-permute-start | bytes 393224 | tf_op jit(solution)/shard_map/ppermute | solution.py:276
  10.0 6.4 %collective-permute-start = (bf16[2,64,512]{2,1,0:T(8,128)(2,1)}, bf16[2,64,512]{2,1,0:T(8,128)(2,1)S(1)}, u32[]{:S(2)}, u32[]{:S(2)}) collective-permute-start(bf16[2,64,512]{2,1,0:T(8,128)(2,1)} %get-tuple-element.40), channel_id=1, source_target_pairs={{0,4},{4,0},{8,12},{12,8},{16,20},{20,16},{24,28},{28,24},{1,5},{5... | collective-permute-start | bytes 393224 | tf_op jit(solution)/shard_map/ppermute | solution.py:276
  10.6 8.3 %collective-permute-start.1 = (bf16[2,64,512]{2,1,0:T(8,128)(2,1)}, bf16[2,64,512]{2,1,0:T(8,128)(2,1)S(1)}, u32[]{:S(2)}, u32[]{:S(2)}) collective-permute-start(bf16[2,64,512]{2,1,0:T(8,128)(2,1)} %get-tuple-element.41), channel_id=1, source_target_pairs={{0,8},{4,12},{8,0},{12,4},{16,24},{20,28},{24,16},{28,20},{1,9},{5... | collective-permute-start | bytes 393224 | tf_op jit(solution)/shard_map/ppermute | solution.py:276
  10.6 12.8 %collective-permute-start.2 = (bf16[2,64,512]{2,1,0:T(8,128)(2,1)}, bf16[2,64,512]{2,1,0:T(8,128)(2,1)S(1)}, u32[]{:S(2)}, u32[]{:S(2)}) collective-permute-start(bf16[2,64,512]{2,1,0:T(8,128)(2,1)} %get-tuple-element.42), channel_id=1, source_target_pairs={{0,12},{4,8},{8,4},{12,0},{16,28},{20,24},{24,20},{28,16},{1,13},{... | collective-permute-start | bytes 393224 | tf_op jit(solution)/shard_map/ppermute | solution.py:276
  13.6 55.5 %copy-start = (bf16[2,64,512]{2,1,0:T(8,128)(2,1)}, bf16[2,64,512]{2,1,0:T(8,128)(2,1)S(1)}, u32[]{:S(2)}) copy-start(bf16[2,64,512]{2,1,0:T(8,128)(2,1)S(1)} %collective-permute-done.7.refs_4_) | copy-start | bytes 393220
  13.6 17.6 %collective-permute-start.3 = (bf16[2,64,512]{2,1,0:T(8,128)(2,1)}, bf16[2,64,512]{2,1,0:T(8,128)(2,1)S(1)}, u32[]{:S(2)}, u32[]{:S(2)}) collective-permute-start(bf16[2,64,512]{2,1,0:T(8,128)(2,1)} %get-tuple-element.43), channel_id=1, source_target_pairs={{0,16},{4,20},{8,24},{12,28},{16,0},{20,4},{24,8},{28,12},{1,17},{... | collective-permute-start | bytes 393224 | tf_op jit(solution)/shard_map/ppermute | solution.py:276
  16.2 52.9 %copy-start.1 = (bf16[2,64,512]{2,1,0:T(8,128)(2,1)}, bf16[2,64,512]{2,1,0:T(8,128)(2,1)S(1)}, u32[]{:S(2)}) copy-start(bf16[2,64,512]{2,1,0:T(8,128)(2,1)S(1)} %collective-permute-done.8.refs_5_) | copy-start | bytes 393220
  16.2 19.7 %collective-permute-start.4 = (bf16[2,64,512]{2,1,0:T(8,128)(2,1)}, bf16[2,64,512]{2,1,0:T(8,128)(2,1)S(1)}, u32[]{:S(2)}, u32[]{:S(2)}) collective-permute-start(bf16[2,64,512]{2,1,0:T(8,128)(2,1)} %get-tuple-element.44), channel_id=1, source_target_pairs={{0,20},{4,16},{8,28},{12,24},{16,4},{20,0},{24,12},{28,8},{1,21},{... | collective-permute-start | bytes 393224 | tf_op jit(solution)/shard_map/ppermute | solution.py:276
  16.5 19.4 %collective-permute-start.5 = (bf16[2,64,512]{2,1,0:T(8,128)(2,1)}, bf16[2,64,512]{2,1,0:T(8,128)(2,1)S(1)}, u32[]{:S(2)}, u32[]{:S(2)}) collective-permute-start(bf16[2,64,512]{2,1,0:T(8,128)(2,1)} %get-tuple-element.45), channel_id=1, source_target_pairs={{0,24},{4,28},{8,16},{12,20},{16,8},{20,12},{24,0},{28,4},{1,25},{... | collective-permute-start | bytes 393224 | tf_op jit(solution)/shard_map/ppermute | solution.py:276
  18.9 30.6 %collective-permute-start.6 = (bf16[2,64,512]{2,1,0:T(8,128)(2,1)}, bf16[2,64,512]{2,1,0:T(8,128)(2,1)S(1)}, u32[]{:S(2)}, u32[]{:S(2)}) collective-permute-start(bf16[2,64,512]{2,1,0:T(8,128)(2,1)} %get-tuple-element.46), channel_id=1, source_target_pairs={{0,28},{4,24},{8,20},{12,16},{16,12},{20,8},{24,4},{28,0},{1,29},{... | collective-permute-start | bytes 393224 | tf_op jit(solution)/shard_map/ppermute | solution.py:276
  23.5 45.7 %collective-permute-start.9 = (bf16[2,64,512]{2,1,0:T(8,128)(2,1)S(1)}, bf16[2,64,512]{2,1,0:T(8,128)(2,1)S(1)}, u32[]{:S(2)}, u32[]{:S(2)}) collective-permute-start(bf16[2,64,512]{2,1,0:T(8,128)(2,1)S(1)} %copy-done.33), channel_id=1, source_target_pairs={{0,12},{4,8},{8,4},{12,0},{16,28},{20,24},{24,20},{28,16},{1,13},{... | collective-permute-start | bytes 393224 | tf_op jit(solution)/shard_map/ppermute | solution.py:276
  31.2 39.5 %collective-permute-start.10 = (bf16[2,64,512]{2,1,0:T(8,128)(2,1)S(1)}, bf16[2,64,512]{2,1,0:T(8,128)(2,1)S(1)}, u32[]{:S(2)}, u32[]{:S(2)}) collective-permute-start(bf16[2,64,512]{2,1,0:T(8,128)(2,1)S(1)} %copy-done.32), channel_id=1, source_target_pairs={{0,16},{4,20},{8,24},{12,28},{16,0},{20,4},{24,8},{28,12},{1,17},{... | collective-permute-start | bytes 393224 | tf_op jit(solution)/shard_map/ppermute | solution.py:276
  35.8 35.4 %collective-permute-start.11 = (bf16[2,64,512]{2,1,0:T(8,128)(2,1)S(1)}, bf16[2,64,512]{2,1,0:T(8,128)(2,1)S(1)}, u32[]{:S(2)}, u32[]{:S(2)}) collective-permute-start(bf16[2,64,512]{2,1,0:T(8,128)(2,1)S(1)} %copy-done.31), channel_id=1, source_target_pairs={{0,20},{4,16},{8,28},{12,24},{16,4},{20,0},{24,12},{28,8},{1,21},{... | collective-permute-start | bytes 393224 | tf_op jit(solution)/shard_map/ppermute | solution.py:276
  35.9 36.8 %collective-permute-start.12 = (bf16[2,64,512]{2,1,0:T(8,128)(2,1)S(1)}, bf16[2,64,512]{2,1,0:T(8,128)(2,1)S(1)}, u32[]{:S(2)}, u32[]{:S(2)}) collective-permute-start(bf16[2,64,512]{2,1,0:T(8,128)(2,1)S(1)} %copy-done.30), channel_id=1, source_target_pairs={{0,24},{4,28},{8,16},{12,20},{16,8},{20,12},{24,0},{28,4},{1,25},{... | collective-permute-start | bytes 393224 | tf_op jit(solution)/shard_map/ppermute | solution.py:276
  43.9 16.3 %all-to-all-start = ((s32[8,1,3]{2,1,0:T(1,128)}), s32[8,1,3]{2,1,0:T(1,128)S(1)}, u32[]{:S(2)}, u32[]{:S(2)}) async-start(s32[8,1,3]{2,1,0:T(1,128)} %broadcast_in_dim.8), calls=%async_computation | async-start | bytes 8192 | tf_op jit(solution)/shard_map/all_to_all | solution.py:284
  49.5 24.0 %collective-permute-start.13 = (bf16[2,64,512]{2,1,0:T(8,128)(2,1)S(1)}, bf16[2,64,512]{2,1,0:T(8,128)(2,1)S(1)}, u32[]{:S(2)}, u32[]{:S(2)}) collective-permute-start(bf16[2,64,512]{2,1,0:T(8,128)(2,1)S(1)} %copy-done.29), channel_id=1, source_target_pairs={{0,28},{4,24},{8,20},{12,16},{16,12},{20,8},{24,4},{28,0},{1,29},{... | collective-permute-start | bytes 393224 | tf_op jit(solution)/shard_map/ppermute | solution.py:276
  69.1 15.9 %collective-permute-start.21 = (bf16[2,64,512]{2,1,0:T(8,128)(2,1)}, bf16[2,64,512]{2,1,0:T(8,128)(2,1)S(1)}, u32[]{:S(2)}, u32[]{:S(2)}) collective-permute-start(bf16[2,64,512]{2,1,0:T(8,128)(2,1)} %get-tuple-element.68), channel_id=1, source_target_pairs={{0,4},{4,0},{8,12},{12,8},{16,20},{20,16},{24,28},{28,24},{1,5},{5... | collective-permute-start | bytes 393224 | tf_op jit(solution)/shard_map/ppermute | solution.py:276
  70.7 16.1 %collective-permute-start.22 = (bf16[2,64,512]{2,1,0:T(8,128)(2,1)}, bf16[2,64,512]{2,1,0:T(8,128)(2,1)S(1)}, u32[]{:S(2)}, u32[]{:S(2)}) collective-permute-start(bf16[2,64,512]{2,1,0:T(8,128)(2,1)} %get-tuple-element.69), channel_id=1, source_target_pairs={{0,8},{4,12},{8,0},{12,4},{16,24},{20,28},{24,16},{28,20},{1,9},{5... | collective-permute-start | bytes 393224 | tf_op jit(solution)/shard_map/ppermute | solution.py:276
  71.2 17.8 %collective-permute-start.23 = (bf16[2,64,512]{2,1,0:T(8,128)(2,1)}, bf16[2,64,512]{2,1,0:T(8,128)(2,1)S(1)}, u32[]{:S(2)}, u32[]{:S(2)}) collective-permute-start(bf16[2,64,512]{2,1,0:T(8,128)(2,1)} %get-tuple-element.70), channel_id=1, source_target_pairs={{0,12},{4,8},{8,4},{12,0},{16,28},{20,24},{24,20},{28,16},{1,13},{... | collective-permute-start | bytes 393224 | tf_op jit(solution)/shard_map/ppermute | solution.py:276
  72.7 17.8 %collective-permute-start.24 = (bf16[2,64,512]{2,1,0:T(8,128)(2,1)}, bf16[2,64,512]{2,1,0:T(8,128)(2,1)S(1)}, u32[]{:S(2)}, u32[]{:S(2)}) collective-permute-start(bf16[2,64,512]{2,1,0:T(8,128)(2,1)} %get-tuple-element.71), channel_id=1, source_target_pairs={{0,16},{4,20},{8,24},{12,28},{16,0},{20,4},{24,8},{28,12},{1,17},{... | collective-permute-start | bytes 393224 | tf_op jit(solution)/shard_map/ppermute | solution.py:276
  73.6 16.9 %collective-permute-start.25 = (bf16[2,64,512]{2,1,0:T(8,128)(2,1)}, bf16[2,64,512]{2,1,0:T(8,128)(2,1)S(1)}, u32[]{:S(2)}, u32[]{:S(2)}) collective-permute-start(bf16[2,64,512]{2,1,0:T(8,128)(2,1)} %get-tuple-element.72), channel_id=1, source_target_pairs={{0,20},{4,16},{8,28},{12,24},{16,4},{20,0},{24,12},{28,8},{1,21},{... | collective-permute-start | bytes 393224 | tf_op jit(solution)/shard_map/ppermute | solution.py:276
  85.0 7.5 %collective-permute-start.26 = (bf16[2,64,512]{2,1,0:T(8,128)(2,1)S(1)}, bf16[2,64,512]{2,1,0:T(8,128)(2,1)S(1)}, u32[]{:S(2)}, u32[]{:S(2)}) collective-permute-start(bf16[2,64,512]{2,1,0:T(8,128)(2,1)S(1)} %copy-done.35), channel_id=1, source_target_pairs={{0,24},{4,28},{8,16},{12,20},{16,8},{20,12},{24,0},{28,4},{1,25},{... | collective-permute-start | bytes 393224 | tf_op jit(solution)/shard_map/ppermute | solution.py:276
  86.8 8.9 %collective-permute-start.27 = (bf16[2,64,512]{2,1,0:T(8,128)(2,1)S(1)}, bf16[2,64,512]{2,1,0:T(8,128)(2,1)S(1)}, u32[]{:S(2)}, u32[]{:S(2)}) collective-permute-start(bf16[2,64,512]{2,1,0:T(8,128)(2,1)S(1)} %copy-done.34), channel_id=1, source_target_pairs={{0,28},{4,24},{8,20},{12,16},{16,12},{20,8},{24,4},{28,0},{1,29},{... | collective-permute-start | bytes 393224 | tf_op jit(solution)/shard_map/ppermute | solution.py:276
  89.0 11.4 %collective-permute-start.14 = (bf16[2,64,512]{2,1,0:T(8,128)(2,1)}, bf16[2,64,512]{2,1,0:T(8,128)(2,1)S(1)}, u32[]{:S(2)}, u32[]{:S(2)}) collective-permute-start(bf16[2,64,512]{2,1,0:T(8,128)(2,1)} %get-tuple-element.60), channel_id=1, source_target_pairs={{0,4},{4,0},{8,12},{12,8},{16,20},{20,16},{24,28},{28,24},{1,5},{5... | collective-permute-start | bytes 393224 | tf_op jit(solution)/shard_map/ppermute | solution.py:276
  90.5 12.4 %collective-permute-start.15 = (bf16[2,64,512]{2,1,0:T(8,128)(2,1)}, bf16[2,64,512]{2,1,0:T(8,128)(2,1)S(1)}, u32[]{:S(2)}, u32[]{:S(2)}) collective-permute-start(bf16[2,64,512]{2,1,0:T(8,128)(2,1)} %get-tuple-element.61), channel_id=1, source_target_pairs={{0,8},{4,12},{8,0},{12,4},{16,24},{20,28},{24,16},{28,20},{1,9},{5... | collective-permute-start | bytes 393224 | tf_op jit(solution)/shard_map/ppermute | solution.py:276
  90.5 40.3 %collective-permute-start.16 = (bf16[2,64,512]{2,1,0:T(8,128)(2,1)}, bf16[2,64,512]{2,1,0:T(8,128)(2,1)S(1)}, u32[]{:S(2)}, u32[]{:S(2)}) collective-permute-start(bf16[2,64,512]{2,1,0:T(8,128)(2,1)} %get-tuple-element.62), channel_id=1, source_target_pairs={{0,12},{4,8},{8,4},{12,0},{16,28},{20,24},{24,20},{28,16},{1,13},{... | collective-permute-start | bytes 393224 | tf_op jit(solution)/shard_map/ppermute | solution.py:276
  92.5 38.3 %collective-permute-start.17 = (bf16[2,64,512]{2,1,0:T(8,128)(2,1)}, bf16[2,64,512]{2,1,0:T(8,128)(2,1)S(1)}, u32[]{:S(2)}, u32[]{:S(2)}) collective-permute-start(bf16[2,64,512]{2,1,0:T(8,128)(2,1)} %get-tuple-element.63), channel_id=1, source_target_pairs={{0,16},{4,20},{8,24},{12,28},{16,0},{20,4},{24,8},{28,12},{1,17},{... | collective-permute-start | bytes 393224 | tf_op jit(solution)/shard_map/ppermute | solution.py:276
  95.6 35.2 %collective-permute-start.18 = (bf16[2,64,512]{2,1,0:T(8,128)(2,1)}, bf16[2,64,512]{2,1,0:T(8,128)(2,1)S(1)}, u32[]{:S(2)}, u32[]{:S(2)}) collective-permute-start(bf16[2,64,512]{2,1,0:T(8,128)(2,1)} %get-tuple-element.64), channel_id=1, source_target_pairs={{0,20},{4,16},{8,28},{12,24},{16,4},{20,0},{24,12},{28,8},{1,21},{... | collective-permute-start | bytes 393224 | tf_op jit(solution)/shard_map/ppermute | solution.py:276
  100.4 30.5 %collective-permute-start.19 = (bf16[2,64,512]{2,1,0:T(8,128)(2,1)}, bf16[2,64,512]{2,1,0:T(8,128)(2,1)S(1)}, u32[]{:S(2)}, u32[]{:S(2)}) collective-permute-start(bf16[2,64,512]{2,1,0:T(8,128)(2,1)} %get-tuple-element.65), channel_id=1, source_target_pairs={{0,24},{4,28},{8,16},{12,20},{16,8},{20,12},{24,0},{28,4},{1,25},{... | collective-permute-start | bytes 393224 | tf_op jit(solution)/shard_map/ppermute | solution.py:276
  102.9 28.0 %collective-permute-start.20 = (bf16[2,64,512]{2,1,0:T(8,128)(2,1)}, bf16[2,64,512]{2,1,0:T(8,128)(2,1)S(1)}, u32[]{:S(2)}, u32[]{:S(2)}) collective-permute-start(bf16[2,64,512]{2,1,0:T(8,128)(2,1)} %get-tuple-element.66), channel_id=1, source_target_pairs={{0,28},{4,24},{8,20},{12,16},{16,12},{20,8},{24,4},{28,0},{1,29},{... | collective-permute-start | bytes 393224 | tf_op jit(solution)/shard_map/ppermute | solution.py:276
  (34 other events, 737.1 us)
